TPU v7x, 32 devices: a whole 2x2x4 slice. The times are simulated.
32 devices in a mesh: fsdp: 4 (over z), tp: 4 (over y, x), job: 2 (over core).
Axes of the slice: x: 2, y: 2, z: 4, core: 2. Of those that a mesh axis runs over, the one named last changes fastest.
Arguments:
- slopes_in: float32 [128, 128, 1024], P('job', 'fsdp', 'tp'), parts along dimension 0, may hold values from -6 to 6
- moments_in: float32 [128, 128, 1024], P('job', 'fsdp', 'tp'), parts along dimension 0, may hold values from -6 to 6
- weights_in: float32 [128, 128, 1024], P('job', 'fsdp', 'tp'), parts along dimension 0, may hold values from -0.1875 to 0.1875
Outputs:
- new_weights: float32 [128, 128, 1024], P('job', 'fsdp', 'tp'), parts along dimension 0
- new_momentum: float32 [128, 128, 1024], P('job', 'fsdp', 'tp'), parts along dimension 0
There are 2 independent parts, one for each index of `job`. A program takes and returns all parts, laid end to end along the dimension named above; each array names one. Nothing has to cross between parts.
All inputs are finite; a program needn't handle non-finite values.
Results may differ from a plain program's by a relative error of at most 0.00019.
Values sent between devices are 32-bit elements; how exact they have to be, the bound alone decides.
A program may use at most 128 MiB of HBM per device.

v0:
```python
import jax
import jax.numpy as jnp
from jax import lax
from jax.sharding import PartitionSpec as P

ITERS = 5
hold_rate = 0.9
learn_rate = 0.8


def body(slopes_in, moments_in, weights_in):
    new_momentum = hold_rate * moments_in + slopes_in
    moved = lax.all_to_all(new_momentum, "fsdp", split_axis=0, concat_axis=1, tiled=True)
    whole = lax.all_to_all(moved, "tp", split_axis=0, concat_axis=2, tiled=True)
    iterate = whole * lax.rsqrt(jnp.sum(whole * whole, axis=(1, 2), keepdims=True) + 1e-06)
    for step in range(ITERS):
        gram = jnp.einsum("mik,mjk->mij", iterate, iterate, precision=lax.Precision.HIGHEST)
        mixed = -4.775 * gram + 2.0315 * jnp.einsum(
            "mij,mjk->mik", gram, gram, precision=lax.Precision.HIGHEST
        )
        iterate = 3.4445 * iterate + jnp.einsum(
            "mij,mjk->mik", mixed, iterate, precision=lax.Precision.HIGHEST
        )
    iterate = lax.all_to_all(iterate, "tp", split_axis=2, concat_axis=0, tiled=True)
    back = lax.all_to_all(iterate, "fsdp", split_axis=1, concat_axis=0, tiled=True)
    new_weights = weights_in - learn_rate * back
    return (new_weights, new_momentum)


def solution(mesh):
    placed = (P("job", "fsdp", "tp"), P("job", "fsdp", "tp"), P("job", "fsdp", "tp"))
    return jax.shard_map(
        body,
        mesh=mesh,
        in_specs=placed,
        out_specs=(P("job", "fsdp", "tp"), P("job", "fsdp", "tp")),
        check_vma=False,
    )
```

profile of v0, /device:TPU:0, one launch (start us, length us, event | category | flops | bytes accessed | tf_op | source)
XLA Modules:
  0.0 195.7 jit_solution(11048177467592807245)
XLA Ops:
  0.6 2.7 %multiply_add_fusion.5 = f32[64,32,256]{2,1,0:T(8,128)S(1)} fusion(f32[64,32,256]{2,1,0:T(8,128)} %param.3, f32[64,32,256]{2,1,0:T(8,128)} %param.4), kind=kLoop, calls=%fused_computation.8 | loop fusion | flops 1048576 | bytes 6291456 | tf_op jit(solution)/shard_map/add | solution.py:12
  3.3 0.0 copy-start
  3.3 54.3 %all_to_all.63 = f32[64,32,256]{2,1,0:T(8,128)S(1)} all-to-all(f32[64,32,256]{2,1,0:T(8,128)S(1)} %multiply_add_fusion.5), channel_id=1, replica_groups=mesh['fsdp'=4,'tp'=4,'job'=2] {'fsdp'}, dimensions={0} | all-to-all | bytes 4194304 | tf_op jit(solution)/shard_map/all_to_all | solution.py:13
  57.7 0.1 copy.17
  57.8 27.8 %all_to_all.64 = f32[16,128,256]{2,1,0:T(8,128)S(1)} all-to-all(f32[16,128,256]{2,1,0:T(8,128)S(1)} %bitcast.49), channel_id=1, replica_groups=mesh['fsdp'=4,'tp'=4,'job'=2] {'tp'}, dimensions={0} | all-to-all | bytes 4194304 | tf_op jit(solution)/shard_map/all_to_all | solution.py:14
  85.6 0.3 multiply_reduce_fusion
  85.9 0.3 copy.25
  86.2 2.3 %fusion.2 = f32[4,128,128]{2,1,0:T(8,128)S(1)} fusion(f32[4,128,1024]{2,1,0:T(8,128)S(1)} %bitcast.45, f32[4]{0:T(128)S(1)} %add_rsqrt_fusion), kind=kOutput, calls=%fused_computation.11 | convolution fusion | flops 805830656 | bytes 2359312 | tf_op jit(solution)/shard_map/mik,mjk->mij/dot_general | solution.py:17
  88.5 0.4 fusion.10
  88.9 2.2 %multiply_add_fusion.4 = f32[4,128,1024]{2,1,0:T(8,128)S(1)} fusion(f32[4,128,1024]{2,1,0:T(8,128)S(1)} %bitcast.46, f32[4,128,128]{2,1,0:T(8,128)S(1)} %fusion.10, f32[4]{0:T(128)S(1)} %add_rsqrt_fusion), kind=kOutput, calls=%fused_computation.6 | convolution fusion | flops 807403520 | bytes 4456464 | tf_op jit(solution)/shard_map/mij,mjk->mik/dot_general | solution.py:21
  91.1 2.1 %fusion.13 = f32[4,128,128]{2,1,0:T(8,128)S(1)} fusion(f32[4,128,1024]{2,1,0:T(8,128)S(1)} %multiply_add_fusion.4), kind=kOutput, calls=%fused_computation.26 | convolution fusion | flops 805306368 | bytes 2359296 | tf_op jit(solution)/shard_map/mik,mjk->mij/dot_general | solution.py:17
  93.1 0.4 fusion.9
  93.5 2.1 %multiply_add_fusion.3 = f32[4,128,1024]{2,1,0:T(8,128)S(1)} fusion(f32[4,128,1024]{2,1,0:T(8,128)S(1)} %multiply_add_fusion.4, f32[4,128,128]{2,1,0:T(8,128)S(1)} %fusion.9), kind=kOutput, calls=%fused_computation.5 | convolution fusion | flops 806354944 | bytes 4456448 | tf_op jit(solution)/shard_map/mij,mjk->mik/dot_general | solution.py:21
  95.6 2.1 %fusion.14 = f32[4,128,128]{2,1,0:T(8,128)S(1)} fusion(f32[4,128,1024]{2,1,0:T(8,128)S(1)} %multiply_add_fusion.3), kind=kOutput, calls=%fused_computation.27 | convolution fusion | flops 805306368 | bytes 2359296 | tf_op jit(solution)/shard_map/mik,mjk->mij/dot_general | solution.py:17
  97.6 0.4 fusion.8
  98.0 2.3 %multiply_add_fusion.2 = f32[4,128,1024]{2,1,0:T(8,128)S(1)} fusion(f32[4,128,1024]{2,1,0:T(8,128)S(1)} %multiply_add_fusion.3, f32[4,128,128]{2,1,0:T(8,128)S(1)} %fusion.8), kind=kOutput, calls=%fused_computation.4 | convolution fusion | flops 806354944 | bytes 4456448 | tf_op jit(solution)/shard_map/mij,mjk->mik/dot_general | solution.py:21
  100.3 2.0 %fusion.15 = f32[4,128,128]{2,1,0:T(8,128)S(1)} fusion(f32[4,128,1024]{2,1,0:T(8,128)S(1)} %multiply_add_fusion.2), kind=kOutput, calls=%fused_computation.28 | convolution fusion | flops 805306368 | bytes 2359296 | tf_op jit(solution)/shard_map/mik,mjk->mij/dot_general | solution.py:17
  102.4 0.4 fusion.7
  102.7 2.1 %multiply_add_fusion.1 = f32[4,128,1024]{2,1,0:T(8,128)S(1)} fusion(f32[4,128,1024]{2,1,0:T(8,128)S(1)} %multiply_add_fusion.2, f32[4,128,128]{2,1,0:T(8,128)S(1)} %fusion.7), kind=kOutput, calls=%fused_computation.3 | convolution fusion | flops 806354944 | bytes 4456448 | tf_op jit(solution)/shard_map/mij,mjk->mik/dot_general | solution.py:21
  104.8 2.0 %fusion.16 = f32[4,128,128]{2,1,0:T(8,128)S(1)} fusion(f32[4,128,1024]{2,1,0:T(8,128)S(1)} %multiply_add_fusion.1), kind=kOutput, calls=%fused_computation.29 | convolution fusion | flops 805306368 | bytes 2359296 | tf_op jit(solution)/shard_map/mik,mjk->mij/dot_general | solution.py:17
  106.9 0.4 fusion.6
  107.3 2.1 %multiply_add_fusion = f32[4,128,1024]{2,1,0:T(8,128)S(1)} fusion(f32[4,128,1024]{2,1,0:T(8,128)S(1)} %multiply_add_fusion.1, f32[4,128,128]{2,1,0:T(8,128)S(1)} %fusion.6), kind=kOutput, calls=%fused_computation.2 | convolution fusion | flops 806354944 | bytes 4456448 | tf_op jit(solution)/shard_map/mij,mjk->mik/dot_general | solution.py:21
  109.3 1.8 copy.19
  111.2 26.5 %all_to_all.65 = f32[4,128,1024]{1,0,2:T(4,128)S(1)} all-to-all(f32[4,128,1024]{1,0,2:T(4,128)} %copy.19), channel_id=1, replica_groups=mesh['fsdp'=4,'tp'=4,'job'=2] {'tp'}, dimensions={2} | all-to-all | bytes 4194304 | tf_op jit(solution)/shard_map/all_to_all | solution.py:24
  137.6 0.1 copy.20
  137.8 1.8 copy.21
  139.6 2.8 %copy.22 = f32[16,128,256]{2,0,1:T(8,128)S(1)} copy(f32[16,128,256]{2,1,0:T(8,128)} %bitcast.51) | data formatting | bytes 4194304 | tf_op jit(solution)/shard_map/all_to_all | solution.py:24
  142.4 48.6 %all_to_all.66 = f32[16,128,256]{2,0,1:T(8,128)S(1)} all-to-all(f32[16,128,256]{2,0,1:T(8,128)S(1)} %copy.22), channel_id=1, replica_groups=mesh['fsdp'=4,'tp'=4,'job'=2] {'fsdp'}, dimensions={1} | all-to-all | bytes 4194304 | tf_op jit(solution)/shard_map/all_to_all | solution.py:25
  191.0 1.4 copy_multiply_fusion
  192.4 0.1 copy.24
  192.5 1.4 copy-done.1
  194.0 1.7 bitcast_subtract_fusion
  (3 shorter events, 0.0 us)
Async XLA Ops:
  3.3 54.4 %copy-start = (f32[64,32,256]{2,1,0:T(8,128)}, f32[64,32,256]{2,1,0:T(8,128)S(1)}, u32[]{:S(2)}) copy-start(f32[64,32,256]{2,1,0:T(8,128)S(1)} %multiply_add_fusion.5) | copy-start | bytes 6291460
  192.4 1.6 copy-start.1
where the time goes:
time: 196 us
  blocking collectives  157 us (80%)
  matrix products  23 us (12%)
  local copies, waits for them, and re-layouts  8.59 us (4%)
  other arithmetic  6.08 us (3%)
    all_to_all x1, blocking collectives, body(): lax.all_to_all(new_momentum, 'fsdp', split_axis=0, concat_axis=1, tiled=T...  54.3 us
    all_to_all x1, blocking collectives, body(): lax.all_to_all(iterate, 'fsdp', split_axis=1, concat_axis=0, tiled=True)  48.6 us
    all_to_all x1, blocking collectives, body(): whole = lax.all_to_all(moved, 'tp', split_axis=0, concat_axis=2, tiled=True)  27.8 us
    all_to_all x1, blocking collectives, body(): lax.all_to_all(iterate, 'tp', split_axis=2, concat_axis=0, tiled=True)  26.5 us
    dot_general x5, matrix products, body(): jnp.einsum('mij,mjk->mik', mixed, iterate, precision=lax.Precision.HIGHEST)  10.7 us
    dot_general x5, matrix products, body(): jnp.einsum('mik,mjk->mij', iterate, iterate, precision=lax.Precision.HIGH...  10.5 us
    all_to_all x3, local copies, waits for them, and re-layouts, body(): lax.all_to_all(iterate, 'tp', split_axis=2, concat_axis=0, tiled=True)  4.76 us

commit v1 on v0

--- a/solution.py
+++ b/solution.py
@@ -1,3 +1,4 @@
+import functools
 import jax
 import jax.numpy as jnp
 from jax import lax
@@ -6,6 +7,18 @@
 ITERS = 5
 hold_rate = 0.9
 learn_rate = 0.8
+
+
+def grid_derive(m, at_axis, dim_at):
+    far_arr = lax.axis_size("tp")
+    step_out = jnp.split(m, far_arr, axis=at_axis)
+    even = jnp.stack(step_out, 0)
+    z1 = lax.all_to_all(even, "tp", 0, 0)
+    piece_next = jnp.concatenate(z1, dim_at)
+    return piece_next
+
+
+_move_stacks_all = functools.partial(grid_derive, at_axis=2, dim_at=0)
 
 
 def body(slopes_in, moments_in, weights_in):
@@ -21,7 +34,7 @@
         iterate = 3.4445 * iterate + jnp.einsum(
             "mij,mjk->mik", mixed, iterate, precision=lax.Precision.HIGHEST
         )
-    iterate = lax.all_to_all(iterate, "tp", split_axis=2, concat_axis=0, tiled=True)
+    iterate = _move_stacks_all(iterate)
     back = lax.all_to_all(iterate, "fsdp", split_axis=1, concat_axis=0, tiled=True)
     new_weights = weights_in - learn_rate * back
     return (new_weights, new_momentum)

time: 196 us -> 189 us (0.964)
  local copies, waits for them, and re-layouts: 8.59 us -> 3.51 us
    all_to_all x3 -> x0, local copies, waits for them, and re-layouts: 4.76 us -> none  [body(): lax.all_to_all(iterate, 'tp', split_axis=2, concat_axis=0, tiled=True)]
where the time goes in v1:
time: 189 us
  blocking collectives  156 us (83%)
  matrix products  23 us (12%)
  other arithmetic  5.12 us (3%)
  local copies, waits for them, and re-layouts  3.51 us (2%)
    all_to_all x1, blocking collectives, body(): lax.all_to_all(new_momentum, 'fsdp', split_axis=0, concat_axis=1, tiled=T...  54.3 us
    all_to_all x1, blocking collectives, body(): lax.all_to_all(iterate, 'fsdp', split_axis=1, concat_axis=0, tiled=True)  48.6 us
    all_to_all x1, blocking collectives, body(): whole = lax.all_to_all(moved, 'tp', split_axis=0, concat_axis=2, tiled=True)  27.8 us
    all_to_all x1, blocking collectives, grid_derive(): z1 = lax.all_to_all(even, 'tp', 0, 0)  25.4 us
    dot_general x5, matrix products, body(): jnp.einsum('mij,mjk->mik', mixed, iterate, precision=lax.Precision.HIGHEST)  10.7 us
    dot_general x5, matrix products, body(): jnp.einsum('mik,mjk->mij', iterate, iterate, precision=lax.Precision.HIGH...  10.5 us

profile of v1, /device:TPU:0, one launch (start us, length us, event | category | flops | bytes accessed | tf_op | source)
XLA Modules:
  0.0 188.6 jit_solution(16118599072934997705)
XLA Ops:
  0.6 2.7 %multiply_add_fusion.5 = f32[64,32,256]{2,1,0:T(8,128)S(1)} fusion(f32[64,32,256]{2,1,0:T(8,128)} %param.3, f32[64,32,256]{2,1,0:T(8,128)} %param.4), kind=kLoop, calls=%fused_computation.8 | loop fusion | flops 1048576 | bytes 6291456 | tf_op jit(solution)/shard_map/add | solution.py:25
  3.3 0.0 copy-start
  3.3 54.3 %all_to_all.50 = f32[64,32,256]{2,1,0:T(8,128)S(1)} all-to-all(f32[64,32,256]{2,1,0:T(8,128)S(1)} %multiply_add_fusion.5), channel_id=1, replica_groups=mesh['fsdp'=4,'tp'=4,'job'=2] {'fsdp'}, dimensions={0} | all-to-all | bytes 4194304 | tf_op jit(solution)/shard_map/all_to_all | solution.py:26
  57.7 0.2 copy.11
  57.9 27.8 %all_to_all.51 = f32[16,128,256]{2,1,0:T(8,128)S(1)} all-to-all(f32[16,128,256]{2,1,0:T(8,128)S(1)} %bitcast.54), channel_id=1, replica_groups=mesh['fsdp'=4,'tp'=4,'job'=2] {'tp'}, dimensions={0} | all-to-all | bytes 4194304 | tf_op jit(solution)/shard_map/all_to_all | solution.py:27
  85.7 0.3 multiply_reduce_fusion
  86.0 0.2 copy.15
  86.3 2.3 %fusion.2 = f32[4,128,128]{2,1,0:T(8,128)S(1)} fusion(f32[4,128,1024]{2,1,0:T(8,128)S(1)} %bitcast.50, f32[4]{0:T(128)S(1)} %add_rsqrt_fusion), kind=kOutput, calls=%fused_computation.11 | convolution fusion | flops 805830656 | bytes 2359312 | tf_op jit(solution)/shard_map/mik,mjk->mij/dot_general | solution.py:30
  88.5 0.4 fusion.10
  88.9 2.1 %multiply_add_fusion.4 = f32[4,128,1024]{2,1,0:T(8,128)S(1)} fusion(f32[4,128,1024]{2,1,0:T(8,128)S(1)} %bitcast.51, f32[4,128,128]{2,1,0:T(8,128)S(1)} %fusion.10, f32[4]{0:T(128)S(1)} %add_rsqrt_fusion), kind=kOutput, calls=%fused_computation.6 | convolution fusion | flops 807403520 | bytes 4456464 | tf_op jit(solution)/shard_map/mij,mjk->mik/dot_general | solution.py:34
  91.1 2.0 %fusion.13 = f32[4,128,128]{2,1,0:T(8,128)S(1)} fusion(f32[4,128,1024]{2,1,0:T(8,128)S(1)} %multiply_add_fusion.4), kind=kOutput, calls=%fused_computation.31 | convolution fusion | flops 805306368 | bytes 2359296 | tf_op jit(solution)/shard_map/mik,mjk->mij/dot_general | solution.py:30
  93.1 0.4 fusion.9
  93.5 2.1 %multiply_add_fusion.3 = f32[4,128,1024]{2,1,0:T(8,128)S(1)} fusion(f32[4,128,1024]{2,1,0:T(8,128)S(1)} %multiply_add_fusion.4, f32[4,128,128]{2,1,0:T(8,128)S(1)} %fusion.9), kind=kOutput, calls=%fused_computation.5 | convolution fusion | flops 806354944 | bytes 4456448 | tf_op jit(solution)/shard_map/mij,mjk->mik/dot_general | solution.py:34
  95.6 2.0 %fusion.14 = f32[4,128,128]{2,1,0:T(8,128)S(1)} fusion(f32[4,128,1024]{2,1,0:T(8,128)S(1)} %multiply_add_fusion.3), kind=kOutput, calls=%fused_computation.32 | convolution fusion | flops 805306368 | bytes 2359296 | tf_op jit(solution)/shard_map/mik,mjk->mij/dot_general | solution.py:30
  97.6 0.4 fusion.8
  98.0 2.3 %multiply_add_fusion.2 = f32[4,128,1024]{2,1,0:T(8,128)S(1)} fusion(f32[4,128,1024]{2,1,0:T(8,128)S(1)} %multiply_add_fusion.3, f32[4,128,128]{2,1,0:T(8,128)S(1)} %fusion.8), kind=kOutput, calls=%fused_computation.4 | convolution fusion | flops 806354944 | bytes 4456448 | tf_op jit(solution)/shard_map/mij,mjk->mik/dot_general | solution.py:34
  100.3 2.0 %fusion.15 = f32[4,128,128]{2,1,0:T(8,128)S(1)} fusion(f32[4,128,1024]{2,1,0:T(8,128)S(1)} %multiply_add_fusion.2), kind=kOutput, calls=%fused_computation.33 | convolution fusion | flops 805306368 | bytes 2359296 | tf_op jit(solution)/shard_map/mik,mjk->mij/dot_general | solution.py:30
  102.4 0.4 fusion.7
  102.7 2.1 %multiply_add_fusion.1 = f32[4,128,1024]{2,1,0:T(8,128)S(1)} fusion(f32[4,128,1024]{2,1,0:T(8,128)S(1)} %multiply_add_fusion.2, f32[4,128,128]{2,1,0:T(8,128)S(1)} %fusion.7), kind=kOutput, calls=%fused_computation.3 | convolution fusion | flops 806354944 | bytes 4456448 | tf_op jit(solution)/shard_map/mij,mjk->mik/dot_general | solution.py:34
  104.8 2.0 %fusion.16 = f32[4,128,128]{2,1,0:T(8,128)S(1)} fusion(f32[4,128,1024]{2,1,0:T(8,128)S(1)} %multiply_add_fusion.1), kind=kOutput, calls=%fused_computation.34 | convolution fusion | flops 805306368 | bytes 2359296 | tf_op jit(solution)/shard_map/mik,mjk->mij/dot_general | solution.py:30
  106.9 0.4 fusion.6
  107.3 2.1 %multiply_add_fusion = f32[4,128,1024]{2,1,0:T(8,128)S(1)} fusion(f32[4,128,1024]{2,1,0:T(8,128)S(1)} %multiply_add_fusion.1, f32[4,128,128]{2,1,0:T(8,128)S(1)} %fusion.6), kind=kOutput, calls=%fused_computation.2 | convolution fusion | flops 806354944 | bytes 4456448 | tf_op jit(solution)/shard_map/mij,mjk->mik/dot_general | solution.py:34
  109.3 0.2 slice_bitcast_fusion.3
  109.6 0.2 pad_maximum_fusion
  109.8 25.4 %all_to_all.52 = f32[4,4,128,256]{3,2,1,0:T(8,128)S(1)} all-to-all(f32[4,4,128,256]{3,2,1,0:T(8,128)S(1)} %pad_maximum_fusion), channel_id=1, replica_groups=mesh['fsdp'=4,'tp'=4,'job'=2] {'tp'}, dimensions={0} | all-to-all | bytes 4194304 | tf_op jit(solution)/shard_map/all_to_all | solution.py:16
  135.1 1.2 copy.13
  136.3 48.6 %all_to_all.53 = f32[16,128,256]{2,0,1:T(8,128)S(1)} all-to-all(f32[16,128,256]{2,0,1:T(8,128)S(1)} %copy.13), channel_id=1, replica_groups=mesh['fsdp'=4,'tp'=4,'job'=2] {'fsdp'}, dimensions={1} | all-to-all | bytes 4194304 | tf_op jit(solution)/shard_map/all_to_all | solution.py:38
  185.0 0.2 broadcast_multiply_fusion
  185.2 0.0 copy-start.1
  185.3 1.2 copy.14
  186.5 0.4 copy-done.1
  186.8 1.7 bitcast_subtract_fusion
  (2 shorter events, 0.0 us)
Async XLA Ops:
  3.3 54.4 %copy-start = (f32[64,32,256]{2,1,0:T(8,128)}, f32[64,32,256]{2,1,0:T(8,128)S(1)}, u32[]{:S(2)}) copy-start(f32[64,32,256]{2,1,0:T(8,128)S(1)} %multiply_add_fusion.5) | copy-start | bytes 6291460
  185.2 1.6 copy-start.1
